TPU v7x, 32 devices: a whole 2x2x4 slice. The times are simulated.
32 devices in a mesh: seq: 8 (over z, core), head: 4 (over y, x).
Axes of the slice: x: 2, y: 2, z: 4, core: 2. Of those that a mesh axis runs over, the one named last changes fastest.
Arguments:
- queries: bfloat16 [1024, 2048], P('seq', 'head'), may hold values from -192 to 192
- keys: bfloat16 [1024, 512], P('seq', 'head'), may hold values from -5 to 5
- values: bfloat16 [1024, 512], P('seq', 'head'), may hold values from -24 to 24
- segments: int32 [1024], replicated, may hold values from 0 to 5, never falling along the last dimension, each value on 1 to 341 neighbouring positions
- out_weight: bfloat16 [2048, 8192], P(None, 'head'), may hold values from -0.125 to 0.125
Outputs:
- mixed: bfloat16 [1024, 8192], P('seq', 'head')
All inputs are finite; a program needn't handle non-finite values.
Results may differ from a plain program's by a relative error of at most 0.007.
Values may be sent and summed in bfloat16 or wider, within the bound.
A program may use at most 64 MiB of HBM per device.

v0:
```python
import jax
import jax.numpy as jnp
from jax import lax
from jax.sharding import PartitionSpec as P

HD = 128
WIN_BLK = 31
masked_score = -1e30


def passed_along(block, axis, distance):
    devices = range(lax.axis_size(axis))
    route = [(i - distance, i) for i in devices if i - distance in devices]
    return lax.ppermute(block, axis, route)


def allowed_keys(segments, query_pos, query_seg, key_first, key_count, window_len):
    key_pos = key_first + jnp.arange(key_count, dtype=jnp.int32)
    clipped = jnp.clip(key_pos, 0, segments.shape[0] - 1)
    key_seg = jnp.take(segments, clipped)
    allowed = key_pos[None, :] <= query_pos[:, None]
    allowed = allowed & (query_pos[:, None] - key_pos[None, :] < window_len)
    allowed = allowed & (key_pos[None, :] >= 0)
    return allowed & (key_seg[None, :] == query_seg[:, None])


def absorb(carry_state, query_heads, key_piece, value_piece, allowed):
    row_max, row_sum, accum = carry_state
    key_count = key_piece.shape[0]
    kv_heads = query_heads.shape[1]
    key_heads = key_piece.reshape(key_count, kv_heads, HD)
    value_heads = value_piece.reshape(key_count, kv_heads, HD)
    scores = jnp.einsum(
        "tagd,sad->agts", query_heads, key_heads, preferred_element_type=jnp.float32
    )
    scores = jnp.where(allowed[None, None], scores * HD ** (-0.5), masked_score)
    new_max = jnp.maximum(row_max, jnp.max(scores, axis=-1))
    weights = jnp.exp(scores - new_max[..., None])
    factor = jnp.exp(row_max - new_max)
    new_sum = row_sum * factor + jnp.sum(weights, axis=-1)
    update = jnp.einsum(
        "agts,sad->agtd",
        weights.astype(jnp.bfloat16),
        value_heads,
        preferred_element_type=jnp.float32,
    )
    return (new_max, new_sum, accum * factor[..., None] + update)


def on_device(queries, keys, values, segments, out_weight):
    row_count = queries.shape[0]
    kv_width = keys.shape[1]
    kv_heads = kv_width // HD
    group_size = queries.shape[1] // kv_width
    cycle_size = lax.axis_size("seq")
    position = lax.axis_index("seq")
    window_len = WIN_BLK * row_count
    reach_blocks = min(WIN_BLK, cycle_size - 1)
    own_first = position * row_count
    query_pos = own_first + jnp.arange(row_count, dtype=jnp.int32)
    query_seg = lax.dynamic_slice_in_dim(segments, own_first, row_count, 0)
    query_heads = queries.reshape(row_count, kv_heads, group_size, HD)
    start_state = (
        jnp.full((kv_heads, group_size, row_count), masked_score, jnp.float32),
        jnp.zeros((kv_heads, group_size, row_count), jnp.float32),
        jnp.zeros((kv_heads, group_size, row_count, HD), jnp.float32),
    )

    def take_block(carry_state, key_piece, value_piece, key_first):
        allowed = allowed_keys(
            segments, query_pos, query_seg, key_first, key_piece.shape[0], window_len
        )
        return absorb(carry_state, query_heads, key_piece, value_piece, allowed)

    carry_state = take_block(start_state, keys, values, own_first)
    near_keys, near_values = passed_along((keys, values), "seq", 1)
    carry_state = take_block(carry_state, near_keys, near_values, own_first - row_count)
    pair_keys = jnp.concatenate([near_keys, keys], axis=0)
    pair_values = jnp.concatenate([near_values, values], axis=0)

    def pair_turn(turn_index, loop_carry):
        moving_keys, moving_values, inner_state = loop_carry
        moving_keys, moving_values = passed_along((moving_keys, moving_values), "seq", 2)
        key_first = own_first - (2 * turn_index + 3) * row_count
        inner_state = take_block(inner_state, moving_keys, moving_values, key_first)
        return (moving_keys, moving_values, inner_state)

    finished = lax.fori_loop(0, reach_blocks // 2, pair_turn, (pair_keys, pair_values, carry_state))
    carry_state = finished[2]
    row_max, row_sum, accum = carry_state
    attended = (accum / row_sum[..., None]).transpose(2, 0, 1, 3)
    attended = attended.reshape(row_count, queries.shape[1]).astype(jnp.bfloat16)
    mixed = jnp.dot(
        lax.all_gather(attended, "head", axis=1, tiled=True),
        out_weight,
        preferred_element_type=jnp.float32,
    )
    return mixed.astype(jnp.bfloat16)


def solution(mesh):
    return jax.shard_map(
        on_device,
        mesh=mesh,
        in_specs=(P("seq", "head"), P("seq", "head"), P("seq", "head"), P(), P(None, "head")),
        out_specs=P("seq", "head"),
        check_vma=False,
    )
```

profile of v0, /device:TPU:0, one launch (start us, length us, event | category | flops | bytes accessed | tf_op | source)
XLA Modules:
  0.0 60.8 jit_solution(18168356742073294899)
XLA Ops:
  0.0 2.4 %collective-permute-start.2 = (bf16[128,128]{1,0:T(8,128)(2,1)}, bf16[128,128]{1,0:T(8,128)(2,1)S(1)}, u32[]{:S(2)}, u32[]{:S(2)}) collective-permute-start(bf16[128,128]{1,0:T(8,128)(2,1)} %param.10), channel_id=1, source_target_pairs={{0,4},{4,8},{8,12},{12,16},{16,20},{20,24},{24,28},{1,5},{5,9},{9,... | collective-permute-start | bytes 98312 | tf_op jit(solution)/shard_map/ppermute | solution.py:14
  2.4 4.6 %collective-permute-start.3 = (bf16[128,128]{1,0:T(8,128)(2,1)}, bf16[128,128]{1,0:T(8,128)(2,1)S(1)}, u32[]{:S(2)}, u32[]{:S(2)}) collective-permute-start(bf16[128,128]{1,0:T(8,128)(2,1)} %param.11), channel_id=1, source_target_pairs={{0,4},{4,8},{8,12},{12,16},{16,20},{20,24},{24,28},{1,5},{5,9},{9,... | collective-permute-start | bytes 98312 | tf_op jit(solution)/shard_map/ppermute | solution.py:14
  7.1 0.8 %dynamic_slice.3 = s32[128]{0:T(128)S(1)} dynamic-slice(s32[1024]{0:T(1024)} %param.12, s32[]{:T(128)S(6)} %select_n.63), dynamic_slice_sizes={128} | dynamic-slice | bytes 1028 | tf_op jit(solution)/shard_map/dynamic_slice | solution.py:61
  7.8 1.6 %gather_fusion.2 = s32[128]{0:T(128)S(1)} fusion(s32[1024]{0:T(1024)} %param.12, s32[1024]{0:T(1024)S(1)} %pad_clamp_fusion.1), kind=kCustom, calls=%fused_computation.2.clone | custom fusion | bytes 1536 | tf_op jit(solution)/shard_map/jit(_take)/gather | solution.py:20
  9.5 1.6 %gather_fusion.1 = s32[128]{0:T(128)S(1)} fusion(s32[1024]{0:T(1024)} %param.12, s32[1024]{0:T(1024)S(1)} %pad_clamp_fusion.2), kind=kCustom, calls=%fused_computation.clone | custom fusion | bytes 1536 | tf_op jit(solution)/shard_map/jit(_take)/gather | solution.py:20
  11.3 1.1 %fusion.54 = (f32[4,128]{1,0:T(4,128)S(1)}, f32[1,4,128,128]{2,3,1,0:T(8,128)S(1)}) fusion(bf16[128,128]{1,0:T(8,128)(2,1)} %param.10, pred[128,128]{0,1:T(8,128)(4,1)S(1)} %get-tuple-element.284, bf16[128,512]{1,0:T(8,128)(2,1)} %param.9), kind=kOutput, calls=%fused_computation.96 | convolution fusion | flops 16973312 | bytes 444416 | tf_op jit(solution)/shard_map/tagd,sad->agts/dot_general | solution.py:33
  12.4 1.0 %copy.16 = bf16[128,512]{0,1:T(8,128)(2,1)S(1)} copy(bf16[128,512]{1,0:T(8,128)(2,1)} %param.9) | data formatting | bytes 262144 | tf_op args[0]
  13.6 1.1 %fusion.55 = (f32[4,128]{1,0:T(4,128)S(1)}, f32[1,4,128,128]{2,3,1,0:T(8,128)S(1)}) fusion(bf16[128,128]{1,0:T(8,128)(2,1)S(1)} %collective-permute-done.2, pred[128,128]{0,1:T(8,128)(4,1)S(1)} %get-tuple-element.285, bf16[128,512]{1,0:T(8,128)(2,1)} %param.9), kind=kOutput, calls=%fused_computation.97 | convolution fusion | flops 16973312 | bytes 444416 | tf_op jit(solution)/shard_map/tagd,sad->agts/dot_general | solution.py:33
  14.8 1.0 %fusion.19 = f32[4,128,128]{2,1,0:T(8,128)S(1)} fusion(f32[1,4,128,128]{2,3,1,0:T(8,128)S(1)} %get-tuple-element.287, f32[4,128]{1,0:T(4,128)S(1)} %get-tuple-element.278, f32[4,128]{1,0:T(4,128)S(1)} %get-tuple-element.282, f32[4,128]{1,0:T(4,128)S(1)} %get-tuple-element.283, bf16[128,128]{1,0:T(8,128)(2,1)} %param.11), kind=kOutput, calls=%fused_computation.36 | convolution fusion | flops 17039360 | bytes 563200 | tf_op jit(solution)/shard_map/agts,sad->agtd/dot_general | solution.py:41
  15.9 0.8 %pad_maximum_fusion = bf16[256,128]{1,0:T(8,128)(2,1)S(1)} fusion(bf16[128,128]{1,0:T(8,128)(2,1)} %param.10, bf16[128,128]{1,0:T(8,128)(2,1)S(1)} %collective-permute-done.2), kind=kLoop, calls=%fused_computation.58 | loop fusion | flops 131072 | bytes 131072 | tf_op jit(solution)/shard_map/concatenate | solution.py:78
  16.6 0.8 %pad_maximum_fusion.1 = bf16[256,128]{1,0:T(8,128)(2,1)S(1)} fusion(bf16[128,128]{1,0:T(8,128)(2,1)} %param.11, bf16[128,128]{1,0:T(8,128)(2,1)S(1)} %collective-permute-done.3), kind=kLoop, calls=%fused_computation.59 | loop fusion | flops 131072 | bytes 131072 | tf_op jit(solution)/shard_map/concatenate | solution.py:79
  17.6 26.8 %while.23 = (s32[]{:T(128)}, bf16[256,128]{1,0:T(8,128)(2,1)S(1)}, bf16[256,128]{1,0:T(8,128)(2,1)S(1)}, f32[1,4,128]{2,1,0:T(4,128)S(1)}, f32[1,4,128]{2,1,0:T(...) while((s32[]{:T(128)}, bf16[256,128]{1,0:T(8,128)(2,1)S(1)}, ...), condition=%wide.region_7.9_spmd.clone.clone, body=%wide.region_4.8_spmd.clone.clone.sunk | while | flops 68393600 | bytes 3260693 | solution.py:88
  17.6 3.5 %collective-permute-start = (bf16[256,128]{1,0:T(8,128)(2,1)S(1)}, bf16[256,128]{1,0:T(8,128)(2,1)S(1)}, u32[]{:S(2)}, u32[]{:S(2)}) collective-permute-start(bf16[256,128]{1,0:T(8,128)(2,1)S(1)} %get-tuple-element.384), channel_id=1, source_target_pairs={{0,8},{4,12},{8,16},{12,20},{16,24},{20,28},{1,9},{5,13},{9,17},{1... | collective-permute-start | bytes 196616 | tf_op jit(solution)/shard_map/while/body/eval_jaxpr/ppermute | solution.py:14
  21.1 3.5 %collective-permute-start.1 = (bf16[256,128]{1,0:T(8,128)(2,1)S(1)}, bf16[256,128]{1,0:T(8,128)(2,1)S(1)}, u32[]{:S(2)}, u32[]{:S(2)}) collective-permute-start(bf16[256,128]{1,0:T(8,128)(2,1)S(1)} %get-tuple-element.385), channel_id=1, source_target_pairs={{0,8},{4,12},{8,16},{12,20},{16,24},{20,28},{1,9},{5,13},{9,17},{1... | collective-permute-start | bytes 196616 | tf_op jit(solution)/shard_map/while/body/eval_jaxpr/ppermute | solution.py:14
  24.7 1.9 %gather_fusion = s32[256]{0:T(256)S(1)} fusion(s32[1024]{0:T(1024)} %get-tuple-element.404, s32[1024]{0:T(1024)S(1)} %pad_clamp_fusion.4), kind=kCustom, calls=%fused_computation.1.clone.clone.clone.1 | custom fusion | bytes 3072 | tf_op jit(solution)/shard_map/while/body/eval_jaxpr/jit(_take)/gather | solution.py:20
  27.6 3.5 %collective-permute-start = (bf16[256,128]{1,0:T(8,128)(2,1)S(1)}, bf16[256,128]{1,0:T(8,128)(2,1)S(1)}, u32[]{:S(2)}, u32[]{:S(2)}) collective-permute-start(bf16[256,128]{1,0:T(8,128)(2,1)S(1)} %get-tuple-element.384), channel_id=1, source_target_pairs={{0,8},{4,12},{8,16},{12,20},{16,24},{20,28},{1,9},{5,13},{9,17},{1... | collective-permute-start | bytes 196616 | tf_op jit(solution)/shard_map/while/body/eval_jaxpr/ppermute | solution.py:14
  31.1 1.9 %collective-permute-start.1 = (bf16[256,128]{1,0:T(8,128)(2,1)S(1)}, bf16[256,128]{1,0:T(8,128)(2,1)S(1)}, u32[]{:S(2)}, u32[]{:S(2)}) collective-permute-start(bf16[256,128]{1,0:T(8,128)(2,1)S(1)} %get-tuple-element.385), channel_id=1, source_target_pairs={{0,8},{4,12},{8,16},{12,20},{16,24},{20,28},{1,9},{5,13},{9,17},{1... | collective-permute-start | bytes 196616 | tf_op jit(solution)/shard_map/while/body/eval_jaxpr/ppermute | solution.py:14
  33.1 1.9 %gather_fusion = s32[256]{0:T(256)S(1)} fusion(s32[1024]{0:T(1024)} %get-tuple-element.404, s32[1024]{0:T(1024)S(1)} %pad_clamp_fusion.4), kind=kCustom, calls=%fused_computation.1.clone.clone.clone.1 | custom fusion | bytes 3072 | tf_op jit(solution)/shard_map/while/body/eval_jaxpr/jit(_take)/gather | solution.py:20
  36.0 3.5 %collective-permute-start = (bf16[256,128]{1,0:T(8,128)(2,1)S(1)}, bf16[256,128]{1,0:T(8,128)(2,1)S(1)}, u32[]{:S(2)}, u32[]{:S(2)}) collective-permute-start(bf16[256,128]{1,0:T(8,128)(2,1)S(1)} %get-tuple-element.384), channel_id=1, source_target_pairs={{0,8},{4,12},{8,16},{12,20},{16,24},{20,28},{1,9},{5,13},{9,17},{1... | collective-permute-start | bytes 196616 | tf_op jit(solution)/shard_map/while/body/eval_jaxpr/ppermute | solution.py:14
  39.6 1.9 %collective-permute-start.1 = (bf16[256,128]{1,0:T(8,128)(2,1)S(1)}, bf16[256,128]{1,0:T(8,128)(2,1)S(1)}, u32[]{:S(2)}, u32[]{:S(2)}) collective-permute-start(bf16[256,128]{1,0:T(8,128)(2,1)S(1)} %get-tuple-element.385), channel_id=1, source_target_pairs={{0,8},{4,12},{8,16},{12,20},{16,24},{20,28},{1,9},{5,13},{9,17},{1... | collective-permute-start | bytes 196616 | tf_op jit(solution)/shard_map/while/body/eval_jaxpr/ppermute | solution.py:14
  41.6 1.9 %gather_fusion = s32[256]{0:T(256)S(1)} fusion(s32[1024]{0:T(1024)} %get-tuple-element.404, s32[1024]{0:T(1024)S(1)} %pad_clamp_fusion.4), kind=kCustom, calls=%fused_computation.1.clone.clone.clone.1 | custom fusion | bytes 3072 | tf_op jit(solution)/shard_map/while/body/eval_jaxpr/jit(_take)/gather | solution.py:20
  44.1 0.3 fusion.75
  44.7 10.7 %all_gather.3 = bf16[128,2048]{0,1:T(8,128)(2,1)S(1)} all-gather(bf16[128,512]{0,1:T(8,128)(2,1)S(1)} %bitcast.142), channel_id=1, replica_groups=mesh['seq'=8,'head'=4] {'head'}, dimensions={1}, use_global_device_ids=true | all-gather | bytes 655360 | tf_op jit(solution)/shard_map/all_gather | solution.py:94
  55.3 5.5 %convolution_convert_fusion = bf16[128,2048]{1,0:T(8,128)(2,1)} fusion(bf16[128,2048]{0,1:T(8,128)(2,1)S(1)} %all_gather.3, bf16[2048,2048]{1,0:T(8,128)(2,1)} %param.13), kind=kOutput, calls=%fused_computation.32 | convolution fusion | flops 1074003968 | bytes 9437184 | tf_op jit(solution)/shard_map/dot_general | solution.py:93
  (65 shorter events, 3.3 us)
Async XLA Ops:
  0.0 13.6 %collective-permute-start.2 = (bf16[128,128]{1,0:T(8,128)(2,1)}, bf16[128,128]{1,0:T(8,128)(2,1)S(1)}, u32[]{:S(2)}, u32[]{:S(2)}) collective-permute-start(bf16[128,128]{1,0:T(8,128)(2,1)} %param.10), channel_id=1, source_target_pairs={{0,4},{4,8},{8,12},{12,16},{16,20},{20,24},{24,28},{1,5},{5,9},{9,... | collective-permute-start | bytes 98312 | tf_op jit(solution)/shard_map/ppermute | solution.py:14
  2.4 14.2 %collective-permute-start.3 = (bf16[128,128]{1,0:T(8,128)(2,1)}, bf16[128,128]{1,0:T(8,128)(2,1)S(1)}, u32[]{:S(2)}, u32[]{:S(2)}) collective-permute-start(bf16[128,128]{1,0:T(8,128)(2,1)} %param.11), channel_id=1, source_target_pairs={{0,4},{4,8},{8,12},{12,16},{16,20},{20,24},{24,28},{1,5},{5,9},{9,... | collective-permute-start | bytes 98312 | tf_op jit(solution)/shard_map/ppermute | solution.py:14
  17.6 9.2 %collective-permute-start = (bf16[256,128]{1,0:T(8,128)(2,1)S(1)}, bf16[256,128]{1,0:T(8,128)(2,1)S(1)}, u32[]{:S(2)}, u32[]{:S(2)}) collective-permute-start(bf16[256,128]{1,0:T(8,128)(2,1)S(1)} %get-tuple-element.384), channel_id=1, source_target_pairs={{0,8},{4,12},{8,16},{12,20},{16,24},{20,28},{1,9},{5,13},{9,17},{1... | collective-permute-start | bytes 196616 | tf_op jit(solution)/shard_map/while/body/eval_jaxpr/ppermute | solution.py:14
  21.1 6.1 %collective-permute-start.1 = (bf16[256,128]{1,0:T(8,128)(2,1)S(1)}, bf16[256,128]{1,0:T(8,128)(2,1)S(1)}, u32[]{:S(2)}, u32[]{:S(2)}) collective-permute-start(bf16[256,128]{1,0:T(8,128)(2,1)S(1)} %get-tuple-element.385), channel_id=1, source_target_pairs={{0,8},{4,12},{8,16},{12,20},{16,24},{20,28},{1,9},{5,13},{9,17},{1... | collective-permute-start | bytes 196616 | tf_op jit(solution)/shard_map/while/body/eval_jaxpr/ppermute | solution.py:14
  27.6 7.7 %collective-permute-start = (bf16[256,128]{1,0:T(8,128)(2,1)S(1)}, bf16[256,128]{1,0:T(8,128)(2,1)S(1)}, u32[]{:S(2)}, u32[]{:S(2)}) collective-permute-start(bf16[256,128]{1,0:T(8,128)(2,1)S(1)} %get-tuple-element.384), channel_id=1, source_target_pairs={{0,8},{4,12},{8,16},{12,20},{16,24},{20,28},{1,9},{5,13},{9,17},{1... | collective-permute-start | bytes 196616 | tf_op jit(solution)/shard_map/while/body/eval_jaxpr/ppermute | solution.py:14
  31.1 4.5 %collective-permute-start.1 = (bf16[256,128]{1,0:T(8,128)(2,1)S(1)}, bf16[256,128]{1,0:T(8,128)(2,1)S(1)}, u32[]{:S(2)}, u32[]{:S(2)}) collective-permute-start(bf16[256,128]{1,0:T(8,128)(2,1)S(1)} %get-tuple-element.385), channel_id=1, source_target_pairs={{0,8},{4,12},{8,16},{12,20},{16,24},{20,28},{1,9},{5,13},{9,17},{1... | collective-permute-start | bytes 196616 | tf_op jit(solution)/shard_map/while/body/eval_jaxpr/ppermute | solution.py:14
  36.0 7.7 %collective-permute-start = (bf16[256,128]{1,0:T(8,128)(2,1)S(1)}, bf16[256,128]{1,0:T(8,128)(2,1)S(1)}, u32[]{:S(2)}, u32[]{:S(2)}) collective-permute-start(bf16[256,128]{1,0:T(8,128)(2,1)S(1)} %get-tuple-element.384), channel_id=1, source_target_pairs={{0,8},{4,12},{8,16},{12,20},{16,24},{20,28},{1,9},{5,13},{9,17},{1... | collective-permute-start | bytes 196616 | tf_op jit(solution)/shard_map/while/body/eval_jaxpr/ppermute | solution.py:14
  39.6 4.6 %collective-permute-start.1 = (bf16[256,128]{1,0:T(8,128)(2,1)S(1)}, bf16[256,128]{1,0:T(8,128)(2,1)S(1)}, u32[]{:S(2)}, u32[]{:S(2)}) collective-permute-start(bf16[256,128]{1,0:T(8,128)(2,1)S(1)} %get-tuple-element.385), channel_id=1, source_target_pairs={{0,8},{4,12},{8,16},{12,20},{16,24},{20,28},{1,9},{5,13},{9,17},{1... | collective-permute-start | bytes 196616 | tf_op jit(solution)/shard_map/while/body/eval_jaxpr/ppermute | solution.py:14
where the time goes:
time: 61.6 us; the launch traced here: 60.8 us
  starting transfers between devices  24.9 us (40%)
  local copies, waits for them, and re-layouts  11.1 us (18%)
  blocking collectives  10.7 us (17%)
  matrix products  10.6 us (17%)
  other arithmetic  2.91 us (5%)
    ppermute x8, starting transfers between devices, passed_along(): return lax.ppermute(block, axis, route)  24.9 us
    all_gather x1, blocking collectives, on_device(): lax.all_gather(attended, 'head', axis=1, tiled=True)  10.7 us
    gather x5, local copies, waits for them, and re-layouts, allowed_keys(): key_seg = jnp.take(segments, clipped)  9.02 us
    dot_general x1, matrix products, on_device(): jnp.dot(lax.all_gather(attended, 'head', axis=1, tiled=True), out_weight,...  5.47 us
    dot_general x5, matrix products, absorb(): jnp.einsum('tagd,sad->agts', query_heads, key_heads, preferred_element_ty...  2.97 us
    dot_general x5, matrix products, absorb(): jnp.einsum('agts,sad->agtd', weights.astype(jnp.bfloat16), value_heads, p...  2.2 us
  transfers between devices with their start and end apart: 8, of which 0 were waited for; matrix products, arithmetic and copies ran while one was open for 28% of the time, Pallas kernels for 0%

commit v1 on v0

--- a/solution.py
+++ b/solution.py
@@ -1,3 +1,4 @@
+import functools
 import jax
 import jax.numpy as jnp
 from jax import lax
@@ -6,6 +7,13 @@
 HD = 128
 WIN_BLK = 31
 masked_score = -1e30
+
+
+def arrays_lift(tile_in, link_axis):
+    return jnp.concatenate(jax.lax.all_gather(tile_in, link_axis), axis=1)
+
+
+bring_desk = functools.partial(arrays_lift, link_axis="head")
 
 
 def passed_along(block, axis, distance):
@@ -90,11 +98,7 @@
     row_max, row_sum, accum = carry_state
     attended = (accum / row_sum[..., None]).transpose(2, 0, 1, 3)
     attended = attended.reshape(row_count, queries.shape[1]).astype(jnp.bfloat16)
-    mixed = jnp.dot(
-        lax.all_gather(attended, "head", axis=1, tiled=True),
-        out_weight,
-        preferred_element_type=jnp.float32,
-    )
+    mixed = jnp.dot(bring_desk(attended), out_weight, preferred_element_type=jnp.float32)
     return mixed.astype(jnp.bfloat16)
 
 

time: 61.6 us -> 62 us (level)
  no operation moved by 1% of the time
where the time goes in v1:
time: 62 us; the launch traced here: 61.2 us
  starting transfers between devices  24.9 us (40%)
  local copies, waits for them, and re-layouts  11.5 us (19%)
  blocking collectives  10.7 us (17%)
  matrix products  10.6 us (17%)
  other arithmetic  2.91 us (5%)
    ppermute x8, starting transfers between devices, passed_along(): return lax.ppermute(block, axis, route)  24.9 us
    all_gather x1, blocking collectives, arrays_lift(): return jnp.concatenate(jax.lax.all_gather(tile_in, link_axis), axis=1)  10.7 us
    gather x5, local copies, waits for them, and re-layouts, allowed_keys(): key_seg = jnp.take(segments, clipped)  9.02 us
    dot_general x1, matrix products, on_device(): jnp.dot(bring_desk(attended), out_weight, preferred_element_type=jnp.floa...  5.47 us
    dot_general x5, matrix products, absorb(): jnp.einsum('tagd,sad->agts', query_heads, key_heads, preferred_element_ty...  2.97 us
    dot_general x5, matrix products, absorb(): jnp.einsum('agts,sad->agtd', weights.astype(jnp.bfloat16), value_heads, p...  2.2 us
  transfers between devices with their start and end apart: 8, of which 0 were waited for; matrix products, arithmetic and copies ran while one was open for 28% of the time, Pallas kernels for 0%

profile of v1, /device:TPU:0, one launch (start us, length us, event | category | flops | bytes accessed | tf_op | source)
XLA Modules:
  0.0 61.2 jit_solution(8540363599064115750)
XLA Ops:
  0.0 2.4 %collective-permute-start.2 = (bf16[128,128]{1,0:T(8,128)(2,1)}, bf16[128,128]{1,0:T(8,128)(2,1)S(1)}, u32[]{:S(2)}, u32[]{:S(2)}) collective-permute-start(bf16[128,128]{1,0:T(8,128)(2,1)} %param.10), channel_id=1, source_target_pairs={{0,4},{4,8},{8,12},{12,16},{16,20},{20,24},{24,28},{1,5},{5,9},{9,... | collective-permute-start | bytes 98312 | tf_op jit(solution)/shard_map/ppermute | solution.py:22
  2.4 4.6 %collective-permute-start.3 = (bf16[128,128]{1,0:T(8,128)(2,1)}, bf16[128,128]{1,0:T(8,128)(2,1)S(1)}, u32[]{:S(2)}, u32[]{:S(2)}) collective-permute-start(bf16[128,128]{1,0:T(8,128)(2,1)} %param.11), channel_id=1, source_target_pairs={{0,4},{4,8},{8,12},{12,16},{16,20},{20,24},{24,28},{1,5},{5,9},{9,... | collective-permute-start | bytes 98312 | tf_op jit(solution)/shard_map/ppermute | solution.py:22
  7.1 0.8 %dynamic_slice.3 = s32[128]{0:T(128)S(1)} dynamic-slice(s32[1024]{0:T(1024)} %param.12, s32[]{:T(128)S(6)} %select_n.63), dynamic_slice_sizes={128} | dynamic-slice | bytes 1028 | tf_op jit(solution)/shard_map/dynamic_slice | solution.py:69
  7.8 1.6 %gather_fusion.2 = s32[128]{0:T(128)S(1)} fusion(s32[1024]{0:T(1024)} %param.12, s32[1024]{0:T(1024)S(1)} %pad_clamp_fusion.1), kind=kCustom, calls=%fused_computation.2.clone | custom fusion | bytes 1536 | tf_op jit(solution)/shard_map/jit(_take)/gather | solution.py:28
  9.5 1.6 %gather_fusion.1 = s32[128]{0:T(128)S(1)} fusion(s32[1024]{0:T(1024)} %param.12, s32[1024]{0:T(1024)S(1)} %pad_clamp_fusion.2), kind=kCustom, calls=%fused_computation.clone | custom fusion | bytes 1536 | tf_op jit(solution)/shard_map/jit(_take)/gather | solution.py:28
  11.3 1.1 %fusion.54 = (f32[4,128]{1,0:T(4,128)S(1)}, f32[1,4,128,128]{2,3,1,0:T(8,128)S(1)}) fusion(bf16[128,128]{1,0:T(8,128)(2,1)} %param.10, pred[128,128]{0,1:T(8,128)(4,1)S(1)} %get-tuple-element.294, bf16[128,512]{1,0:T(8,128)(2,1)} %param.9), kind=kOutput, calls=%fused_computation.96 | convolution fusion | flops 16973312 | bytes 444416 | tf_op jit(solution)/shard_map/tagd,sad->agts/dot_general | solution.py:41
  12.4 1.0 %copy.24 = bf16[128,512]{0,1:T(8,128)(2,1)S(1)} copy(bf16[128,512]{1,0:T(8,128)(2,1)} %param.9) | data formatting | bytes 262144 | tf_op args[0]
  13.6 1.1 %fusion.55 = (f32[4,128]{1,0:T(4,128)S(1)}, f32[1,4,128,128]{2,3,1,0:T(8,128)S(1)}) fusion(bf16[128,128]{1,0:T(8,128)(2,1)S(1)} %collective-permute-done.2, pred[128,128]{0,1:T(8,128)(4,1)S(1)} %get-tuple-element.295, bf16[128,512]{1,0:T(8,128)(2,1)} %param.9), kind=kOutput, calls=%fused_computation.97 | convolution fusion | flops 16973312 | bytes 444416 | tf_op jit(solution)/shard_map/tagd,sad->agts/dot_general | solution.py:41
  14.8 1.0 %fusion.19 = f32[4,128,128]{2,1,0:T(8,128)S(1)} fusion(f32[1,4,128,128]{2,3,1,0:T(8,128)S(1)} %get-tuple-element.297, f32[4,128]{1,0:T(4,128)S(1)} %get-tuple-element.288, f32[4,128]{1,0:T(4,128)S(1)} %get-tuple-element.292, f32[4,128]{1,0:T(4,128)S(1)} %get-tuple-element.293, bf16[128,128]{1,0:T(8,128)(2,1)} %param.11), kind=kOutput, calls=%fused_computation.36 | convolution fusion | flops 17039360 | bytes 563200 | tf_op jit(solution)/shard_map/agts,sad->agtd/dot_general | solution.py:49
  15.9 0.8 %pad_maximum_fusion = bf16[256,128]{1,0:T(8,128)(2,1)S(1)} fusion(bf16[128,128]{1,0:T(8,128)(2,1)} %param.10, bf16[128,128]{1,0:T(8,128)(2,1)S(1)} %collective-permute-done.2), kind=kLoop, calls=%fused_computation.58 | loop fusion | flops 131072 | bytes 131072 | tf_op jit(solution)/shard_map/concatenate | solution.py:86
  16.6 0.8 %pad_maximum_fusion.1 = bf16[256,128]{1,0:T(8,128)(2,1)S(1)} fusion(bf16[128,128]{1,0:T(8,128)(2,1)} %param.11, bf16[128,128]{1,0:T(8,128)(2,1)S(1)} %collective-permute-done.3), kind=kLoop, calls=%fused_computation.59 | loop fusion | flops 131072 | bytes 131072 | tf_op jit(solution)/shard_map/concatenate | solution.py:87
  17.6 26.8 %while.23 = (s32[]{:T(128)}, bf16[256,128]{1,0:T(8,128)(2,1)S(1)}, bf16[256,128]{1,0:T(8,128)(2,1)S(1)}, f32[1,4,128]{2,1,0:T(4,128)S(1)}, f32[1,4,128]{2,1,0:T(...) while((s32[]{:T(128)}, bf16[256,128]{1,0:T(8,128)(2,1)S(1)}, ...), condition=%wide.region_7.9_spmd.clone.clone, body=%wide.region_4.8_spmd.clone.clone.sunk | while | flops 68393600 | bytes 3260693 | solution.py:96
  17.6 3.5 %collective-permute-start = (bf16[256,128]{1,0:T(8,128)(2,1)S(1)}, bf16[256,128]{1,0:T(8,128)(2,1)S(1)}, u32[]{:S(2)}, u32[]{:S(2)}) collective-permute-start(bf16[256,128]{1,0:T(8,128)(2,1)S(1)} %get-tuple-element.394), channel_id=1, source_target_pairs={{0,8},{4,12},{8,16},{12,20},{16,24},{20,28},{1,9},{5,13},{9,17},{1... | collective-permute-start | bytes 196616 | tf_op jit(solution)/shard_map/while/body/eval_jaxpr/ppermute | solution.py:22
  21.1 3.5 %collective-permute-start.1 = (bf16[256,128]{1,0:T(8,128)(2,1)S(1)}, bf16[256,128]{1,0:T(8,128)(2,1)S(1)}, u32[]{:S(2)}, u32[]{:S(2)}) collective-permute-start(bf16[256,128]{1,0:T(8,128)(2,1)S(1)} %get-tuple-element.395), channel_id=1, source_target_pairs={{0,8},{4,12},{8,16},{12,20},{16,24},{20,28},{1,9},{5,13},{9,17},{1... | collective-permute-start | bytes 196616 | tf_op jit(solution)/shard_map/while/body/eval_jaxpr/ppermute | solution.py:22
  24.7 1.9 %gather_fusion = s32[256]{0:T(256)S(1)} fusion(s32[1024]{0:T(1024)} %get-tuple-element.414, s32[1024]{0:T(1024)S(1)} %pad_clamp_fusion.4), kind=kCustom, calls=%fused_computation.1.clone.clone.clone.1 | custom fusion | bytes 3072 | tf_op jit(solution)/shard_map/while/body/eval_jaxpr/jit(_take)/gather | solution.py:28
  27.6 3.5 %collective-permute-start = (bf16[256,128]{1,0:T(8,128)(2,1)S(1)}, bf16[256,128]{1,0:T(8,128)(2,1)S(1)}, u32[]{:S(2)}, u32[]{:S(2)}) collective-permute-start(bf16[256,128]{1,0:T(8,128)(2,1)S(1)} %get-tuple-element.394), channel_id=1, source_target_pairs={{0,8},{4,12},{8,16},{12,20},{16,24},{20,28},{1,9},{5,13},{9,17},{1... | collective-permute-start | bytes 196616 | tf_op jit(solution)/shard_map/while/body/eval_jaxpr/ppermute | solution.py:22
  31.1 1.9 %collective-permute-start.1 = (bf16[256,128]{1,0:T(8,128)(2,1)S(1)}, bf16[256,128]{1,0:T(8,128)(2,1)S(1)}, u32[]{:S(2)}, u32[]{:S(2)}) collective-permute-start(bf16[256,128]{1,0:T(8,128)(2,1)S(1)} %get-tuple-element.395), channel_id=1, source_target_pairs={{0,8},{4,12},{8,16},{12,20},{16,24},{20,28},{1,9},{5,13},{9,17},{1... | collective-permute-start | bytes 196616 | tf_op jit(solution)/shard_map/while/body/eval_jaxpr/ppermute | solution.py:22
  33.1 1.9 %gather_fusion = s32[256]{0:T(256)S(1)} fusion(s32[1024]{0:T(1024)} %get-tuple-element.414, s32[1024]{0:T(1024)S(1)} %pad_clamp_fusion.4), kind=kCustom, calls=%fused_computation.1.clone.clone.clone.1 | custom fusion | bytes 3072 | tf_op jit(solution)/shard_map/while/body/eval_jaxpr/jit(_take)/gather | solution.py:28
  36.0 3.5 %collective-permute-start = (bf16[256,128]{1,0:T(8,128)(2,1)S(1)}, bf16[256,128]{1,0:T(8,128)(2,1)S(1)}, u32[]{:S(2)}, u32[]{:S(2)}) collective-permute-start(bf16[256,128]{1,0:T(8,128)(2,1)S(1)} %get-tuple-element.394), channel_id=1, source_target_pairs={{0,8},{4,12},{8,16},{12,20},{16,24},{20,28},{1,9},{5,13},{9,17},{1... | collective-permute-start | bytes 196616 | tf_op jit(solution)/shard_map/while/body/eval_jaxpr/ppermute | solution.py:22
  39.6 1.9 %collective-permute-start.1 = (bf16[256,128]{1,0:T(8,128)(2,1)S(1)}, bf16[256,128]{1,0:T(8,128)(2,1)S(1)}, u32[]{:S(2)}, u32[]{:S(2)}) collective-permute-start(bf16[256,128]{1,0:T(8,128)(2,1)S(1)} %get-tuple-element.395), channel_id=1, source_target_pairs={{0,8},{4,12},{8,16},{12,20},{16,24},{20,28},{1,9},{5,13},{9,17},{1... | collective-permute-start | bytes 196616 | tf_op jit(solution)/shard_map/while/body/eval_jaxpr/ppermute | solution.py:22
  41.6 1.9 %gather_fusion = s32[256]{0:T(256)S(1)} fusion(s32[1024]{0:T(1024)} %get-tuple-element.414, s32[1024]{0:T(1024)S(1)} %pad_clamp_fusion.4), kind=kCustom, calls=%fused_computation.1.clone.clone.clone.1 | custom fusion | bytes 3072 | tf_op jit(solution)/shard_map/while/body/eval_jaxpr/jit(_take)/gather | solution.py:28
  44.1 0.3 fusion.75
  44.8 10.7 %all_gather.4 = bf16[4,128,512]{2,1,0:T(8,128)(2,1)S(1)} all-gather(bf16[1,128,512]{2,1,0:T(8,128)(2,1)S(1)} %copy.27), channel_id=1, replica_groups=mesh['seq'=8,'head'=4] {'head'}, dimensions={0}, use_global_device_ids=true | all-gather | bytes 655360 | tf_op jit(solution)/shard_map/all_gather | solution.py:13
  55.7 5.5 %convolution_convert_fusion = bf16[128,2048]{1,0:T(8,128)(2,1)} fusion(bf16[128,2048]{0,1:T(8,128)(2,1)S(1)} %bitcast.143, bf16[2048,2048]{1,0:T(8,128)(2,1)} %param.13), kind=kOutput, calls=%fused_computation.32 | convolution fusion | flops 1074003968 | bytes 9437184 | tf_op jit(solution)/shard_map/dot_general | solution.py:101
  (67 shorter events, 3.7 us)
Async XLA Ops:
  0.0 13.6 %collective-permute-start.2 = (bf16[128,128]{1,0:T(8,128)(2,1)}, bf16[128,128]{1,0:T(8,128)(2,1)S(1)}, u32[]{:S(2)}, u32[]{:S(2)}) collective-permute-start(bf16[128,128]{1,0:T(8,128)(2,1)} %param.10), channel_id=1, source_target_pairs={{0,4},{4,8},{8,12},{12,16},{16,20},{20,24},{24,28},{1,5},{5,9},{9,... | collective-permute-start | bytes 98312 | tf_op jit(solution)/shard_map/ppermute | solution.py:22
  2.4 14.2 %collective-permute-start.3 = (bf16[128,128]{1,0:T(8,128)(2,1)}, bf16[128,128]{1,0:T(8,128)(2,1)S(1)}, u32[]{:S(2)}, u32[]{:S(2)}) collective-permute-start(bf16[128,128]{1,0:T(8,128)(2,1)} %param.11), channel_id=1, source_target_pairs={{0,4},{4,8},{8,12},{12,16},{16,20},{20,24},{24,28},{1,5},{5,9},{9,... | collective-permute-start | bytes 98312 | tf_op jit(solution)/shard_map/ppermute | solution.py:22
  17.6 9.2 %collective-permute-start = (bf16[256,128]{1,0:T(8,128)(2,1)S(1)}, bf16[256,128]{1,0:T(8,128)(2,1)S(1)}, u32[]{:S(2)}, u32[]{:S(2)}) collective-permute-start(bf16[256,128]{1,0:T(8,128)(2,1)S(1)} %get-tuple-element.394), channel_id=1, source_target_pairs={{0,8},{4,12},{8,16},{12,20},{16,24},{20,28},{1,9},{5,13},{9,17},{1... | collective-permute-start | bytes 196616 | tf_op jit(solution)/shard_map/while/body/eval_jaxpr/ppermute | solution.py:22
  21.1 6.1 %collective-permute-start.1 = (bf16[256,128]{1,0:T(8,128)(2,1)S(1)}, bf16[256,128]{1,0:T(8,128)(2,1)S(1)}, u32[]{:S(2)}, u32[]{:S(2)}) collective-permute-start(bf16[256,128]{1,0:T(8,128)(2,1)S(1)} %get-tuple-element.395), channel_id=1, source_target_pairs={{0,8},{4,12},{8,16},{12,20},{16,24},{20,28},{1,9},{5,13},{9,17},{1... | collective-permute-start | bytes 196616 | tf_op jit(solution)/shard_map/while/body/eval_jaxpr/ppermute | solution.py:22
  27.6 7.7 %collective-permute-start = (bf16[256,128]{1,0:T(8,128)(2,1)S(1)}, bf16[256,128]{1,0:T(8,128)(2,1)S(1)}, u32[]{:S(2)}, u32[]{:S(2)}) collective-permute-start(bf16[256,128]{1,0:T(8,128)(2,1)S(1)} %get-tuple-element.394), channel_id=1, source_target_pairs={{0,8},{4,12},{8,16},{12,20},{16,24},{20,28},{1,9},{5,13},{9,17},{1... | collective-permute-start | bytes 196616 | tf_op jit(solution)/shard_map/while/body/eval_jaxpr/ppermute | solution.py:22
  31.1 4.5 %collective-permute-start.1 = (bf16[256,128]{1,0:T(8,128)(2,1)S(1)}, bf16[256,128]{1,0:T(8,128)(2,1)S(1)}, u32[]{:S(2)}, u32[]{:S(2)}) collective-permute-start(bf16[256,128]{1,0:T(8,128)(2,1)S(1)} %get-tuple-element.395), channel_id=1, source_target_pairs={{0,8},{4,12},{8,16},{12,20},{16,24},{20,28},{1,9},{5,13},{9,17},{1... | collective-permute-start | bytes 196616 | tf_op jit(solution)/shard_map/while/body/eval_jaxpr/ppermute | solution.py:22
  36.0 7.7 %collective-permute-start = (bf16[256,128]{1,0:T(8,128)(2,1)S(1)}, bf16[256,128]{1,0:T(8,128)(2,1)S(1)}, u32[]{:S(2)}, u32[]{:S(2)}) collective-permute-start(bf16[256,128]{1,0:T(8,128)(2,1)S(1)} %get-tuple-element.394), channel_id=1, source_target_pairs={{0,8},{4,12},{8,16},{12,20},{16,24},{20,28},{1,9},{5,13},{9,17},{1... | collective-permute-start | bytes 196616 | tf_op jit(solution)/shard_map/while/body/eval_jaxpr/ppermute | solution.py:22
  39.6 4.6 %collective-permute-start.1 = (bf16[256,128]{1,0:T(8,128)(2,1)S(1)}, bf16[256,128]{1,0:T(8,128)(2,1)S(1)}, u32[]{:S(2)}, u32[]{:S(2)}) collective-permute-start(bf16[256,128]{1,0:T(8,128)(2,1)S(1)} %get-tuple-element.395), channel_id=1, source_target_pairs={{0,8},{4,12},{8,16},{12,20},{16,24},{20,28},{1,9},{5,13},{9,17},{1... | collective-permute-start | bytes 196616 | tf_op jit(solution)/shard_map/while/body/eval_jaxpr/ppermute | solution.py:22
